TPU v7x, 256 devices: a whole 4x4x8 slice. The times are simulated.
256 devices in a mesh: grp: 8 (over y, core), chan: 32 (over z, x).
Axes of the slice: x: 4, y: 4, z: 8, core: 2. Of those that a mesh axis runs over, the one named last changes fastest.
Arguments:
- fibre_records: bfloat16 [2048, 256, 1536], P(('grp', 'chan')), may hold values from -6 to 6
- station_records: bfloat16 [1024, 256, 1536], P('chan'), may hold values from -6 to 6
- band_mask: int32 [8, 256], replicated, may hold values 0 or 1
- station_valid: int32 [1024], P('chan'), may hold values 0 or 1
- segment_keep: int32 [256], replicated, may hold values 0 or 1
Outputs:
- cross_spectra: float32 [2, 8, 2048, 1024], P(None, None, ('grp', 'chan'))
All inputs are finite; a program needn't handle non-finite values. No bound on the sum of `station_valid` on one device may be relied on, other than what follows from the above.
Results may differ from a plain program's by a relative error of at most 0.0072.
Values may be sent and summed in bfloat16 or wider, within the bound.
No kernel may reach another device: no remote copies, remote signals or barrier semaphores. Data moves between devices by JAX's collectives and lax.ppermute only.
A program may use at most 128 MiB of HBM per device.

v0:
```python
import math
import jax
import jax.numpy as jnp
from jax import lax
from jax.sharding import PartitionSpec as P

SEG = 256
SAMPLES = 1536
NFREQ = 8
FIRST_BIN = 24


def laid_out(blocks, dim):
    lengths = list(blocks.shape[1:])
    lengths[dim] *= blocks.shape[0]
    return jnp.moveaxis(blocks, 0, dim).reshape(lengths)


def from_everyone(x, axis):
    copies = jnp.broadcast_to(x, (lax.axis_size(axis), *x.shape))
    return lax.all_to_all(copies, axis, split_axis=0, concat_axis=0, tiled=True)


def collect(x, axis, dim):
    return laid_out(from_everyone(x, axis), dim)


def time_table():
    sample_index = jnp.arange(SAMPLES, dtype=jnp.int32)
    bin_index = FIRST_BIN + jnp.arange(NFREQ, dtype=jnp.int32)
    phase = sample_index[:, None] * bin_index[None, :] % SAMPLES
    angle = phase.astype(jnp.float32) * (2.0 * math.pi / SAMPLES)
    return jnp.concatenate([jnp.cos(angle), -jnp.sin(angle)], axis=1).astype(jnp.bfloat16)


def wave_tables(width):
    index = jnp.arange(width, dtype=jnp.int32)
    phase = index[:, None] * index[None, :] % width
    angle = phase.astype(jnp.float32) * (2.0 * math.pi / width)
    return (jnp.cos(angle).astype(jnp.bfloat16), jnp.sin(angle).astype(jnp.bfloat16))


def matmul(left, right):
    return jnp.dot(left, right, preferred_element_type=jnp.float32)


def wavenumber_filter(spectra, cosines, sines, weights):
    width, count = (spectra.shape[0], spectra.shape[1])
    real_part = spectra[:, :, :NFREQ].reshape(width, count * NFREQ)
    imag_part = spectra[:, :, NFREQ:].reshape(width, count * NFREQ)
    fwd_real = matmul(cosines, real_part) + matmul(sines, imag_part)
    fwd_imag = matmul(cosines, imag_part) - matmul(sines, real_part)
    fwd_real = (
        (fwd_real.reshape(width, count, NFREQ) * weights[:, None, :])
        .astype(jnp.bfloat16)
        .reshape(width, count * NFREQ)
    )
    fwd_imag = (
        (fwd_imag.reshape(width, count, NFREQ) * weights[:, None, :])
        .astype(jnp.bfloat16)
        .reshape(width, count * NFREQ)
    )
    back_real = (matmul(cosines, fwd_real) - matmul(sines, fwd_imag)) / width
    back_imag = (matmul(sines, fwd_real) + matmul(cosines, fwd_imag)) / width
    joined = jnp.concatenate(
        [back_real.reshape(width, count, NFREQ), back_imag.reshape(width, count, NFREQ)], axis=2
    )
    return joined.astype(jnp.bfloat16)


def scale_rows(spectra, totals, valid):
    factor = lax.rsqrt(totals / (2 * SEG * NFREQ) + 1e-06) * valid.astype(jnp.float32)
    return (spectra * factor[:, None, None]).astype(jnp.bfloat16)


def transform(records, dft_table):
    rows, segs = (records.shape[0], records.shape[1])
    return matmul(records.reshape(rows * segs, SAMPLES), dft_table).reshape(rows, segs, 2 * NFREQ)


def pair_spectra(fibre_part, keep_part, band_part):
    kept = fibre_part * keep_part.astype(jnp.bfloat16)[None, :, None]
    fibre_four = kept.reshape(kept.shape[0], kept.shape[1], 2, NFREQ)
    band_four = band_part.reshape(band_part.shape[0], band_part.shape[1], 2, NFREQ)
    rotated = jnp.concatenate([-band_four[:, :, 1:], band_four[:, :, :1]], axis=2)
    real_out = jnp.einsum(
        "cgpb,sgpb->bcs", fibre_four, band_four, preferred_element_type=jnp.float32
    )
    imag_out = jnp.einsum("cgpb,sgpb->bcs", fibre_four, rotated, preferred_element_type=jnp.float32)
    return jnp.stack([real_out, imag_out])


def shards(fibre_records, station_records, band_mask, station_valid, segment_keep):
    dft_table = time_table()
    channels_here = fibre_records.shape[0]
    chan_count = lax.axis_size("chan")
    block_width = channels_here * chan_count
    seg_local = SEG // chan_count
    fibre_spec = transform(fibre_records, dft_table).astype(jnp.bfloat16)
    station_spec = transform(station_records, dft_table)
    totals = jnp.sum(station_spec * station_spec, axis=(1, 2))
    bands_local = scale_rows(station_spec, totals, station_valid)
    cosines, sines = wave_tables(block_width)
    weights = band_mask.T.astype(jnp.float32)
    outgoing = fibre_spec.reshape(channels_here, chan_count, seg_local, 2 * NFREQ)
    arrived = lax.all_to_all(outgoing, "chan", split_axis=1, concat_axis=0, tiled=True)
    width = arrived.shape[0]
    count = arrived.shape[2]
    result = wavenumber_filter(arrived.reshape(width, count, 2 * NFREQ), cosines, sines, weights)
    filtered_block = result.reshape(width, 1, count, 2 * NFREQ)
    filtered_block = filtered_block.reshape(block_width, seg_local, 2 * NFREQ)
    piece = collect(filtered_block, "chan", 1)
    block_cross = pair_spectra(piece, segment_keep, bands_local)
    result = lax.all_to_all(
        block_cross.astype(jnp.bfloat16), "chan", split_axis=2, concat_axis=3, tiled=True
    ).astype(block_cross.dtype)
    return result * (1.0 / math.sqrt(SEG * SAMPLES))


def solution(mesh):
    placed = (P(("grp", "chan"), None, None), P("chan", None, None), P(), P("chan"), P())
    return jax.shard_map(
        shards,
        mesh=mesh,
        in_specs=placed,
        out_specs=P(None, None, ("grp", "chan"), None),
        check_vma=False,
    )
```

profile of v0, /device:TPU:16, one launch (start us, length us, event | category | flops | bytes accessed | tf_op | source)
XLA Modules:
  0.0 125.0 jit_solution(6500059093318800454)
XLA Ops:
  0.0 0.3 cosine_convert_fusion.5
  0.3 4.5 %fusion = bf16[2048,16]{0,1:T(8,128)(2,1)S(1)} fusion(bf16[2048,1536]{1,0:T(8,128)(2,1)} %bitcast.79, bf16[1536,8]{0,1:T(8,128)(2,1)S(1)} %get-tuple-element.10, bf16[1536,8]{0,1:T(8,128)(2,1)S(1)} %get-tuple-element.9), kind=kOutput, calls=%fused_computation.1 | convolution fusion | flops 100794368 | bytes 6406144 | tf_op jit(solution)/shard_map/dot_general | solution.py:44
  5.3 1.2 reshape.69
  6.5 11.3 %all-to-all-start = ((bf16[32,2,512]{2,1,0:T(2,128)(2,1)}), bf16[32,2,512]{2,1,0:T(2,128)(2,1)S(1)}, u32[]{:S(2)}, u32[]{:S(2)}) async-start(bf16[32,2,512]{2,1,0:T(2,128)(2,1)} %reshape.69), calls=%async_computation | async-start | bytes 131072 | tf_op jit(solution)/shard_map/all_to_all | solution.py:106
  17.8 9.9 %all-to-all-done = bf16[32,2,512]{2,1,0:T(2,128)(2,1)S(1)} async-done(((bf16[32,2,512]{2,1,0:T(2,128)(2,1)}), bf16[32,2,512]{2,1,0:T(2,128)(2,1)S(1)}, u32[]{:S(2)}, u32[]{:S(2)}) %all-to-all-start) | async-done | bytes 65568 | tf_op jit(solution)/shard_map/all_to_all | solution.py:106
  27.8 0.4 reshape.70
  28.4 0.3 copy.49
  28.7 1.1 fusion.26
  29.8 0.3 copy.48
  30.1 1.1 fusion.28
  31.2 1.1 fusion.9
  32.3 1.1 fusion.27
  33.4 1.1 fusion.29
  34.5 1.1 fusion.10
  35.6 1.1 fusion.14
  36.7 1.1 fusion.13
  37.8 1.6 %broadcast_in_dim.2 = bf16[32,256,8,16]{1,3,2,0:T(8,128)(2,1)} broadcast(bf16[256,8,16]{0,2,1:T(8,128)(2,1)S(1)} %pad_maximum_fusion.1), dimensions={1,2,3} | broadcast | bytes 2162688 | tf_op jit(solution)/shard_map/broadcast_in_dim | solution.py:20
  39.4 4.3 %all-to-all-start.1 = ((bf16[32,256,8,16]{1,3,2,0:T(8,128)(2,1)}), bf16[32,256,8,16]{1,3,2,0:T(8,128)(2,1)S(1)}, u32[]{:S(2)}, u32[]{:S(2)}) async-start(bf16[32,256,8,16]{1,3,2,0:T(8,128)(2,1)} %broadcast_in_dim.2), calls=%async_computation.1 | async-start | bytes 4194304 | tf_op jit(solution)/shard_map/all_to_all | solution.py:21
  43.8 11.6 %fusion.15 = (f32[8192]{0:T(1024)S(1)}, f32[16,8192]{1,0:T(8,128)S(1)}) fusion(bf16[8192,1536]{1,0:T(8,128)(2,1)} %bitcast.76, bf16[1536,8]{0,1:T(8,128)(2,1)S(1)} %get-tuple-element.10, bf16[1536,8]{0,1:T(8,128)(2,1)S(1)} %get-tuple-element.9), kind=kOutput, calls=%fused_computation.24 | convolution fusion | flops 403005440 | bytes 25772032 | tf_op jit(solution)/shard_map/dot_general | solution.py:44
  55.7 37.7 %all-to-all-done.1 = bf16[32,256,8,16]{1,3,2,0:T(8,128)(2,1)S(1)} async-done(((bf16[32,256,8,16]{1,3,2,0:T(8,128)(2,1)}), bf16[32,256,8,16]{1,3,2,0:T(8,128)(2,1)S(1)}, u32[]{:S(2)}, u32[]{:S(2)}) %all-to-all-start.1) | async-done | bytes 2097184 | tf_op jit(solution)/shard_map/all_to_all | solution.py:21
  93.4 1.7 %broadcast_multiply_fusion = bf16[256,256,2,8]{0,3,2,1:T(8,128)(2,1)} fusion(bf16[256,256,2,8]{0,3,2,1:T(8,128)(2,1)S(1)} %bitcast.78, bf16[256]{0:T(256)(128)(2,1)S(1)} %convert_element_type.94), kind=kLoop, calls=%fused_computation.22 | loop fusion | flops 1048576 | bytes 4194816 | tf_op jit(solution)/shard_map/mul | solution.py:82
  95.1 3.0 %copy.51 = bf16[256,256,2,8]{1,0,2,3:T(8,128)(2,1)S(1)} copy(bf16[256,256,2,8]{0,3,2,1:T(8,128)(2,1)} %broadcast_multiply_fusion) | data formatting | bytes 4194304 | tf_op jit(solution)/shard_map/mul | solution.py:82
  98.1 0.7 fusion.4
  98.8 0.7 fusion.3
  99.6 0.9 copy.53
  100.5 1.0 reshape.71
  101.5 16.7 %all_to_all.29 = bf16[32,2,2048]{2,1,0:T(2,128)(2,1)S(1)} all-to-all(bf16[32,2,2048]{2,1,0:T(2,128)(2,1)S(1)} %reshape.71), channel_id=1, replica_groups=mesh['grp'=8,'chan'=32] {'chan'}, dimensions={0} | all-to-all | bytes 524288 | tf_op jit(solution)/shard_map/all_to_all | solution.py:114
  118.2 0.5 reshape.72
  118.7 0.8 copy.54
  119.6 0.6 copy.55
  120.2 1.7 %copy.56 = f32[2,8,8,32,32]{4,3,2,1,0:T(8,128)} copy(f32[2,8,8,32,32]{4,2,3,1,0:T(8,128)S(1)} %bitcast.77) | data formatting | bytes 1048576 | tf_op jit(solution)/shard_map/mul | solution.py:117
  122.0 3.1 %mul.184 = f32[2,8,8,1024]{3,2,1,0:T(8,128)} reshape(f32[2,8,8,32,32]{4,3,2,1,0:T(8,128)} %copy.56) | data formatting | bytes 1048576 | tf_op jit(solution)/shard_map/mul | solution.py:117
  (20 shorter events, 1.1 us)
Async XLA Ops:
  4.8 13.0 %copy-start = (s32[8,256]{1,0:T(8,128)S(1)}, s32[8,256]{1,0:T(8,128)}, u32[]{:S(2)}) copy-start(s32[8,256]{1,0:T(8,128)} %param.7) | copy-start | bytes 24580
  6.5 21.3 %all-to-all-start = ((bf16[32,2,512]{2,1,0:T(2,128)(2,1)}), bf16[32,2,512]{2,1,0:T(2,128)(2,1)S(1)}, u32[]{:S(2)}, u32[]{:S(2)}) async-start(bf16[32,2,512]{2,1,0:T(2,128)(2,1)} %reshape.69), calls=%async_computation | async-start | bytes 131072 | tf_op jit(solution)/shard_map/all_to_all | solution.py:106
  39.4 4.3 %copy-start.1 = (s32[256]{0:T(256)S(1)}, s32[256]{0:T(256)}, u32[]{:S(2)}) copy-start(s32[256]{0:T(256)} %param.9) | copy-start | bytes 3076
  39.4 54.0 %all-to-all-start.1 = ((bf16[32,256,8,16]{1,3,2,0:T(8,128)(2,1)}), bf16[32,256,8,16]{1,3,2,0:T(8,128)(2,1)S(1)}, u32[]{:S(2)}, u32[]{:S(2)}) async-start(bf16[32,256,8,16]{1,3,2,0:T(8,128)(2,1)} %broadcast_in_dim.2), calls=%async_computation.1 | async-start | bytes 4194304 | tf_op jit(solution)/shard_map/all_to_all | solution.py:21
  43.8 11.7 %copy-start.2 = (s32[32]{0:T(128)S(1)}, s32[32]{0:T(128)}, u32[]{:S(2)}) copy-start(s32[32]{0:T(128)} %param.8) | copy-start | bytes 388
where the time goes:
time: 125 us
  waiting for transfers between devices  47.6 us (38%)
  matrix products  26.3 us (21%)
  blocking collectives  16.7 us (13%)
  local copies, waits for them, and re-layouts  16.1 us (13%)
  starting transfers between devices  15.6 us (12%)
  other arithmetic  2.44 us (2%)
    all_to_all x1, waiting for transfers between devices, from_everyone(): return lax.all_to_all(copies, axis, split_axis=0, concat_axis=0, tiled=True)  37.7 us
    dot_general x10, matrix products, matmul(): return jnp.dot(left, right, preferred_element_type=jnp.float32)  24.9 us
    all_to_all x1, blocking collectives, shards(): lax.all_to_all(block_cross.astype(jnp.bfloat16), 'chan', split_axis=2, co...  16.7 us
    all_to_all x1, starting transfers between devices, shards(): lax.all_to_all(outgoing, 'chan', split_axis=1, concat_axis=0, tiled=True)  11.3 us
    all_to_all x1, waiting for transfers between devices, shards(): lax.all_to_all(outgoing, 'chan', split_axis=1, concat_axis=0, tiled=True)  9.95 us
    mul x3, local copies, waits for them, and re-layouts, shards(): return result * (1.0 / math.sqrt(SEG * SAMPLES))  5.38 us
    all_to_all x1, starting transfers between devices, from_everyone(): return lax.all_to_all(copies, axis, split_axis=0, concat_axis=0, tiled=True)  4.32 us
    unnamed x10, local copies, waits for them, and re-layouts  3.11 us
  transfers between devices with their start and end apart: 2, of which 2 were waited for; matrix products, arithmetic and copies ran while one was open for 10% of the time, Pallas kernels for 0%

commit v1 on v0

--- a/solution.py
+++ b/solution.py
@@ -111,8 +111,14 @@
     filtered_block = filtered_block.reshape(block_width, seg_local, 2 * NFREQ)
     piece = collect(filtered_block, "chan", 1)
     block_cross = pair_spectra(piece, segment_keep, bands_local)
-    result = lax.all_to_all(
-        block_cross.astype(jnp.bfloat16), "chan", split_axis=2, concat_axis=3, tiled=True
+    result = jnp.concatenate(
+        lax.all_to_all(
+            jnp.stack(jnp.split(block_cross.astype(jnp.bfloat16), lax.axis_size("chan"), axis=2)),
+            "chan",
+            0,
+            0,
+        ),
+        axis=3,
     ).astype(block_cross.dtype)
     return result * (1.0 / math.sqrt(SEG * SAMPLES))
 

time: 125 us -> 149 us (1.19)
  local copies, waits for them, and re-layouts: 16.1 us -> 35.9 us
  other arithmetic: 2.44 us -> 5.68 us
    another operation x1 -> x33, local copies, waits for them, and re-layouts: 0.95 us -> 22.8 us  [shards(): jnp.stack(jnp.split(block_cross.astype(jnp.bfloat16), lax.axis_size('chan...]
    another operation x2 -> x5, other arithmetic: 0.33 us -> 3.36 us  [the longest x4 3.07 us: shards(): jnp.stack(jnp.split(block_cross.astype(jnp.bfloat16), lax.axis_size('chan...]
    mul x3 -> x2, local copies, waits for them, and re-layouts: 5.38 us -> 2.96 us  [shards(): return result * (1.0 / math.sqrt(SEG * SAMPLES))]
    unnamed x10 -> x67, local copies, waits for them, and re-layouts: 3.11 us -> 4.26 us
  transfers between devices with their start and end apart: 2 -> 2, of which waited for: 2 -> 2; matrix products, arithmetic and copies ran while one was open for 10% -> 8% of each run, Pallas kernels for 0% -> 0%
where the time goes in v1:
time: 149 us; the launch traced here: 148 us
  waiting for transfers between devices  47.6 us (32%)
  local copies, waits for them, and re-layouts  35.9 us (24%)
  matrix products  26.3 us (18%)
  blocking collectives  16.7 us (11%)
  starting transfers between devices  15.6 us (10%)
  other arithmetic  5.68 us (4%)
    all_to_all x1, waiting for transfers between devices, from_everyone(): return lax.all_to_all(copies, axis, split_axis=0, concat_axis=0, tiled=True)  37.7 us
    dot_general x10, matrix products, matmul(): return jnp.dot(left, right, preferred_element_type=jnp.float32)  24.9 us
    another operation x33, local copies, waits for them, and re-layouts, shards(): jnp.stack(jnp.split(block_cross.astype(jnp.bfloat16), lax.axis_size('chan...  22.8 us
    all_to_all x1, blocking collectives, shards(): lax.all_to_all(jnp.stack(jnp.split(block_cross.astype(jnp.bfloat16), lax....  16.7 us
    all_to_all x1, starting transfers between devices, shards(): lax.all_to_all(outgoing, 'chan', split_axis=1, concat_axis=0, tiled=True)  11.3 us
    all_to_all x1, waiting for transfers between devices, shards(): lax.all_to_all(outgoing, 'chan', split_axis=1, concat_axis=0, tiled=True)  9.95 us
    all_to_all x1, starting transfers between devices, from_everyone(): return lax.all_to_all(copies, axis, split_axis=0, concat_axis=0, tiled=True)  4.32 us
    unnamed x67, local copies, waits for them, and re-layouts  4.26 us
  transfers between devices with their start and end apart: 2, of which 2 were waited for; matrix products, arithmetic and copies ran while one was open for 8% of the time, Pallas kernels for 0%

profile of v1, /device:TPU:16, one launch (start us, length us, event | category | flops | bytes accessed | tf_op | source)
XLA Modules:
  0.0 148.4 jit_solution(17311059230770294558)
XLA Ops:
  0.3 4.5 %fusion = bf16[2048,16]{0,1:T(8,128)(2,1)S(1)} fusion(bf16[2048,1536]{1,0:T(8,128)(2,1)} %bitcast.139, bf16[1536,8]{0,1:T(8,128)(2,1)S(1)} %get-tuple-element.42, bf16[1536,8]{0,1:T(8,128)(2,1)S(1)} %get-tuple-element.41), kind=kOutput, calls=%fused_computation.1 | convolution fusion | flops 100794368 | bytes 6406144 | tf_op jit(solution)/shard_map/dot_general | solution.py:44
  5.3 1.2 reshape.68
  6.5 11.3 %all-to-all-start = ((bf16[32,2,512]{2,1,0:T(2,128)(2,1)}), bf16[32,2,512]{2,1,0:T(2,128)(2,1)S(1)}, u32[]{:S(2)}, u32[]{:S(2)}) async-start(bf16[32,2,512]{2,1,0:T(2,128)(2,1)} %reshape.68), calls=%async_computation | async-start | bytes 131072 | tf_op jit(solution)/shard_map/all_to_all | solution.py:106
  17.8 9.9 %all-to-all-done = bf16[32,2,512]{2,1,0:T(2,128)(2,1)S(1)} async-done(((bf16[32,2,512]{2,1,0:T(2,128)(2,1)}), bf16[32,2,512]{2,1,0:T(2,128)(2,1)S(1)}, u32[]{:S(2)}, u32[]{:S(2)}) %all-to-all-start) | async-done | bytes 65568 | tf_op jit(solution)/shard_map/all_to_all | solution.py:106
  31.2 1.1 fusion.9
  33.4 1.1 fusion.92
  34.5 1.1 fusion.10
  35.6 1.1 fusion.14
  36.7 1.1 fusion.13
  37.8 1.6 %broadcast_in_dim.2 = bf16[32,256,8,16]{1,3,2,0:T(8,128)(2,1)} broadcast(bf16[256,8,16]{0,2,1:T(8,128)(2,1)S(1)} %pad_maximum_fusion.1), dimensions={1,2,3} | broadcast | bytes 2162688 | tf_op jit(solution)/shard_map/broadcast_in_dim | solution.py:20
  39.4 4.3 %all-to-all-start.1 = ((bf16[32,256,8,16]{1,3,2,0:T(8,128)(2,1)}), bf16[32,256,8,16]{1,3,2,0:T(8,128)(2,1)S(1)}, u32[]{:S(2)}, u32[]{:S(2)}) async-start(bf16[32,256,8,16]{1,3,2,0:T(8,128)(2,1)} %broadcast_in_dim.2), calls=%async_computation.1 | async-start | bytes 4194304 | tf_op jit(solution)/shard_map/all_to_all | solution.py:21
  43.7 11.6 %fusion.15 = (f32[8192]{0:T(1024)S(1)}, f32[16,8192]{1,0:T(8,128)S(1)}) fusion(bf16[8192,1536]{1,0:T(8,128)(2,1)} %bitcast.137, bf16[1536,8]{0,1:T(8,128)(2,1)S(1)} %get-tuple-element.42, bf16[1536,8]{0,1:T(8,128)(2,1)S(1)} %get-tuple-element.41), kind=kOutput, calls=%fused_computation.87 | convolution fusion | flops 403005440 | bytes 25772032 | tf_op jit(solution)/shard_map/dot_general | solution.py:44
  55.7 37.7 %all-to-all-done.1 = bf16[32,256,8,16]{1,3,2,0:T(8,128)(2,1)S(1)} async-done(((bf16[32,256,8,16]{1,3,2,0:T(8,128)(2,1)}), bf16[32,256,8,16]{1,3,2,0:T(8,128)(2,1)S(1)}, u32[]{:S(2)}, u32[]{:S(2)}) %all-to-all-start.1) | async-done | bytes 2097184 | tf_op jit(solution)/shard_map/all_to_all | solution.py:21
  93.4 1.7 %broadcast_multiply_fusion = bf16[256,256,2,8]{0,3,2,1:T(8,128)(2,1)} fusion(bf16[256,256,2,8]{0,3,2,1:T(8,128)(2,1)S(1)} %bitcast.138, bf16[256]{0:T(256)(128)(2,1)S(1)} %convert_element_type.93), kind=kLoop, calls=%fused_computation.85 | loop fusion | flops 1048576 | bytes 4194816 | tf_op jit(solution)/shard_map/mul | solution.py:82
  95.1 3.0 %copy.61 = bf16[256,256,2,8]{1,0,2,3:T(8,128)(2,1)S(1)} copy(bf16[256,256,2,8]{0,3,2,1:T(8,128)(2,1)} %broadcast_multiply_fusion) | data formatting | bytes 4194304 | tf_op jit(solution)/shard_map/mul | solution.py:82
  99.5 1.3 fusion.88
  100.8 1.2 fusion.27
  104.1 1.6 %copy.64 = bf16[1,2,8,8,32]{4,3,2,1,0:T(8,128)(2,1)} copy(bf16[1,2,8,8,32]{3,4,2,1,0:T(8,128)(2,1)} %get-tuple-element.9) | data formatting | bytes 16384 | tf_op jit(solution)/shard_map/stack | solution.py:116
  105.7 1.6 %copy.65 = bf16[1,2,8,8,32]{4,3,2,1,0:T(8,128)(2,1)} copy(bf16[1,2,8,8,32]{3,4,2,1,0:T(8,128)(2,1)} %get-tuple-element.10) | data formatting | bytes 16384 | tf_op jit(solution)/shard_map/stack | solution.py:116
  107.3 1.6 %copy.66 = bf16[1,2,8,8,32]{4,3,2,1,0:T(8,128)(2,1)} copy(bf16[1,2,8,8,32]{3,4,2,1,0:T(8,128)(2,1)} %get-tuple-element.11) | data formatting | bytes 16384 | tf_op jit(solution)/shard_map/stack | solution.py:116
  108.9 1.6 %copy.67 = bf16[1,2,8,8,32]{4,3,2,1,0:T(8,128)(2,1)} copy(bf16[1,2,8,8,32]{3,4,2,1,0:T(8,128)(2,1)} %get-tuple-element.12) | data formatting | bytes 16384 | tf_op jit(solution)/shard_map/stack | solution.py:116
  110.5 1.6 %copy.68 = bf16[1,2,8,8,32]{4,3,2,1,0:T(8,128)(2,1)} copy(bf16[1,2,8,8,32]{3,4,2,1,0:T(8,128)(2,1)} %get-tuple-element.13) | data formatting | bytes 16384 | tf_op jit(solution)/shard_map/stack | solution.py:116
  112.1 1.6 %copy.69 = bf16[1,2,8,8,32]{4,3,2,1,0:T(8,128)(2,1)} copy(bf16[1,2,8,8,32]{3,4,2,1,0:T(8,128)(2,1)} %get-tuple-element.14) | data formatting | bytes 16384 | tf_op jit(solution)/shard_map/stack | solution.py:116
  113.8 1.6 %copy.70 = bf16[1,2,8,8,32]{4,3,2,1,0:T(8,128)(2,1)} copy(bf16[1,2,8,8,32]{3,4,2,1,0:T(8,128)(2,1)} %get-tuple-element.15) | data formatting | bytes 16384 | tf_op jit(solution)/shard_map/stack | solution.py:116
  115.4 1.6 %copy.71 = bf16[1,2,8,8,32]{4,3,2,1,0:T(8,128)(2,1)} copy(bf16[1,2,8,8,32]{3,4,2,1,0:T(8,128)(2,1)} %get-tuple-element.17) | data formatting | bytes 16384 | tf_op jit(solution)/shard_map/stack | solution.py:116
  117.0 1.6 %copy.72 = bf16[1,2,8,8,32]{4,3,2,1,0:T(8,128)(2,1)} copy(bf16[1,2,8,8,32]{3,4,2,1,0:T(8,128)(2,1)} %get-tuple-element.18) | data formatting | bytes 16384 | tf_op jit(solution)/shard_map/stack | solution.py:116
  118.6 1.6 %copy.73 = bf16[1,2,8,8,32]{4,3,2,1,0:T(8,128)(2,1)} copy(bf16[1,2,8,8,32]{3,4,2,1,0:T(8,128)(2,1)} %get-tuple-element.19) | data formatting | bytes 16384 | tf_op jit(solution)/shard_map/stack | solution.py:116
  120.2 1.6 %copy.74 = bf16[1,2,8,8,32]{4,3,2,1,0:T(8,128)(2,1)} copy(bf16[1,2,8,8,32]{3,4,2,1,0:T(8,128)(2,1)} %get-tuple-element.20) | data formatting | bytes 16384 | tf_op jit(solution)/shard_map/stack | solution.py:116
  121.8 1.6 %copy.75 = bf16[1,2,8,8,32]{4,3,2,1,0:T(8,128)(2,1)} copy(bf16[1,2,8,8,32]{3,4,2,1,0:T(8,128)(2,1)} %get-tuple-element.21) | data formatting | bytes 16384 | tf_op jit(solution)/shard_map/stack | solution.py:116
  128.0 16.7 %all_to_all.25 = bf16[32,2,2048]{2,1,0:T(2,128)(2,1)S(1)} all-to-all(bf16[32,2,2048]{2,1,0:T(2,128)(2,1)S(1)} %reshape.70), channel_id=1, replica_groups=mesh['grp'=8,'chan'=32] {'chan'}, dimensions={0} | all-to-all | bytes 524288 | tf_op jit(solution)/shard_map/all_to_all | solution.py:115
  145.5 1.2 copy.95
  146.7 1.7 %mul.180 = f32[2,8,8,1024]{3,2,1,0:T(8,128)} reshape(f32[2,8,8,32,32]{4,3,2,1,0:T(8,128)S(1)} %copy.95) | data formatting | bytes 1048576 | tf_op jit(solution)/shard_map/mul | solution.py:123
  (110 shorter events, 14.0 us)
Async XLA Ops:
  4.8 13.0 %copy-start.13 = (s32[8,256]{1,0:T(8,128)S(1)}, s32[8,256]{1,0:T(8,128)}, u32[]{:S(2)}) copy-start(s32[8,256]{1,0:T(8,128)} %param.7) | copy-start | bytes 24580
  6.5 21.3 %all-to-all-start = ((bf16[32,2,512]{2,1,0:T(2,128)(2,1)}), bf16[32,2,512]{2,1,0:T(2,128)(2,1)S(1)}, u32[]{:S(2)}, u32[]{:S(2)}) async-start(bf16[32,2,512]{2,1,0:T(2,128)(2,1)} %reshape.68), calls=%async_computation | async-start | bytes 131072 | tf_op jit(solution)/shard_map/all_to_all | solution.py:106
  39.4 4.3 %copy-start.14 = (s32[256]{0:T(256)S(1)}, s32[256]{0:T(256)}, u32[]{:S(2)}) copy-start(s32[256]{0:T(256)} %param.9) | copy-start | bytes 3076
  39.4 54.0 %all-to-all-start.1 = ((bf16[32,256,8,16]{1,3,2,0:T(8,128)(2,1)}), bf16[32,256,8,16]{1,3,2,0:T(8,128)(2,1)S(1)}, u32[]{:S(2)}, u32[]{:S(2)}) async-start(bf16[32,256,8,16]{1,3,2,0:T(8,128)(2,1)} %broadcast_in_dim.2), calls=%async_computation.1 | async-start | bytes 4194304 | tf_op jit(solution)/shard_map/all_to_all | solution.py:21
  43.7 11.7 %copy-start.15 = (s32[32]{0:T(128)S(1)}, s32[32]{0:T(128)}, u32[]{:S(2)}) copy-start(s32[32]{0:T(128)} %param.8) | copy-start | bytes 388
  124.2 2.5 %copy-start.2 = (bf16[1,2,8,8,32]{4,3,2,1,0:T(8,128)(2,1)S(1)}, bf16[1,2,8,8,32]{4,3,2,1,0:T(8,128)(2,1)}, u32[]{:S(2)}) copy-start(bf16[1,2,8,8,32]{4,3,2,1,0:T(8,128)(2,1)} %copy.74) | copy-start | bytes 24580
  124.2 2.5 %copy-start.1 = (bf16[1,2,8,8,32]{4,3,2,1,0:T(8,128)(2,1)S(1)}, bf16[1,2,8,8,32]{4,3,2,1,0:T(8,128)(2,1)}, u32[]{:S(2)}) copy-start(bf16[1,2,8,8,32]{4,3,2,1,0:T(8,128)(2,1)} %copy.75) | copy-start | bytes 24580
  124.2 2.5 %copy-start = (bf16[1,2,8,8,32]{4,3,2,1,0:T(8,128)(2,1)S(1)}, bf16[1,2,8,8,32]{4,3,2,1,0:T(8,128)(2,1)}, u32[]{:S(2)}) copy-start(bf16[1,2,8,8,32]{4,3,2,1,0:T(8,128)(2,1)} %copy.76) | copy-start | bytes 24580
  124.3 2.3 %copy-start.5 = (bf16[1,2,8,8,32]{4,3,2,1,0:T(8,128)(2,1)S(1)}, bf16[1,2,8,8,32]{4,3,2,1,0:T(8,128)(2,1)}, u32[]{:S(2)}) copy-start(bf16[1,2,8,8,32]{4,3,2,1,0:T(8,128)(2,1)} %copy.71) | copy-start | bytes 24580
  124.3 2.3 %copy-start.4 = (bf16[1,2,8,8,32]{4,3,2,1,0:T(8,128)(2,1)S(1)}, bf16[1,2,8,8,32]{4,3,2,1,0:T(8,128)(2,1)}, u32[]{:S(2)}) copy-start(bf16[1,2,8,8,32]{4,3,2,1,0:T(8,128)(2,1)} %copy.72) | copy-start | bytes 24580
  124.3 2.3 %copy-start.3 = (bf16[1,2,8,8,32]{4,3,2,1,0:T(8,128)(2,1)S(1)}, bf16[1,2,8,8,32]{4,3,2,1,0:T(8,128)(2,1)}, u32[]{:S(2)}) copy-start(bf16[1,2,8,8,32]{4,3,2,1,0:T(8,128)(2,1)} %copy.73) | copy-start | bytes 24580
  124.4 2.1 %copy-start.8 = (bf16[1,2,8,8,32]{4,3,2,1,0:T(8,128)(2,1)S(1)}, bf16[1,2,8,8,32]{4,3,2,1,0:T(8,128)(2,1)}, u32[]{:S(2)}) copy-start(bf16[1,2,8,8,32]{4,3,2,1,0:T(8,128)(2,1)} %copy.68) | copy-start | bytes 24580
  124.4 2.1 %copy-start.7 = (bf16[1,2,8,8,32]{4,3,2,1,0:T(8,128)(2,1)S(1)}, bf16[1,2,8,8,32]{4,3,2,1,0:T(8,128)(2,1)}, u32[]{:S(2)}) copy-start(bf16[1,2,8,8,32]{4,3,2,1,0:T(8,128)(2,1)} %copy.69) | copy-start | bytes 24580
  124.4 2.1 %copy-start.6 = (bf16[1,2,8,8,32]{4,3,2,1,0:T(8,128)(2,1)S(1)}, bf16[1,2,8,8,32]{4,3,2,1,0:T(8,128)(2,1)}, u32[]{:S(2)}) copy-start(bf16[1,2,8,8,32]{4,3,2,1,0:T(8,128)(2,1)} %copy.70) | copy-start | bytes 24580
  124.6 1.8 %copy-start.11 = (bf16[1,2,8,8,32]{4,3,2,1,0:T(8,128)(2,1)S(1)}, bf16[1,2,8,8,32]{4,3,2,1,0:T(8,128)(2,1)}, u32[]{:S(2)}) copy-start(bf16[1,2,8,8,32]{4,3,2,1,0:T(8,128)(2,1)} %copy.64) | copy-start | bytes 24580
  124.6 1.8 %copy-start.10 = (bf16[1,2,8,8,32]{4,3,2,1,0:T(8,128)(2,1)S(1)}, bf16[1,2,8,8,32]{4,3,2,1,0:T(8,128)(2,1)}, u32[]{:S(2)}) copy-start(bf16[1,2,8,8,32]{4,3,2,1,0:T(8,128)(2,1)} %copy.66) | copy-start | bytes 24580
  124.6 1.9 %copy-start.9 = (bf16[1,2,8,8,32]{4,3,2,1,0:T(8,128)(2,1)S(1)}, bf16[1,2,8,8,32]{4,3,2,1,0:T(8,128)(2,1)}, u32[]{:S(2)}) copy-start(bf16[1,2,8,8,32]{4,3,2,1,0:T(8,128)(2,1)} %copy.67) | copy-start | bytes 24580
  124.7 1.7 %copy-start.12 = (bf16[1,2,8,8,32]{4,3,2,1,0:T(8,128)(2,1)S(1)}, bf16[1,2,8,8,32]{4,3,2,1,0:T(8,128)(2,1)}, u32[]{:S(2)}) copy-start(bf16[1,2,8,8,32]{4,3,2,1,0:T(8,128)(2,1)} %copy.65) | copy-start | bytes 24580
